TPU v7x, 512 devices: a 4x2x32 block of a 4x8x32 slice. The times are simulated.
512 devices in a mesh: groups: 2 (over y), ep: 32 (over z), tp: 4 (over x), dp: 2 (over core).
Axes of the slice: x: 4, y: 2, z: 32, core: 2. Of those that a mesh axis runs over, the one named last changes fastest.
The devices are a block of a 4x8x32 slice.
Arguments:
- tokens: bfloat16 [4096, 5120], P(('groups', 'ep', 'tp', 'dp')), parts along dimension 0, may hold values from -6 to 6
- route_weights: float32 [4096, 8], P(('groups', 'ep', 'tp', 'dp')), parts along dimension 0, may hold values from 0.1 to 1
- expert_ids: int32 [4096, 8], P(('groups', 'ep', 'tp', 'dp')), parts along dimension 0, may hold values from 0 to 31, all different within a row; in each aligned block of 8 rows (0 to 7, 8 to 15, ...) at most 4 rows name the same one
- gate_weight: bfloat16 [32, 5120, 1024], P('ep', None, ('tp', 'dp')), may hold values from -0.078125 to 0.078125
- up_weight: bfloat16 [32, 5120, 1024], P('ep', None, ('tp', 'dp')), may hold values from -0.078125 to 0.078125
- down_weight: bfloat16 [32, 1024, 5120], P('ep', None, ('tp', 'dp')), may hold values from -0.1875 to 0.1875
Outputs:
- combined: bfloat16 [4096, 5120], P(('groups', 'ep', 'tp', 'dp')), parts along dimension 0
There are 2 independent parts, one for each index of `groups`. A program takes and returns all parts, laid end to end along the dimension named above; an argument that names none is the same for every part. Nothing has to cross between parts.
Inputs may be any that keep to these rules, and one draw needn't show every extreme that they name: `expert_ids`: each row names 8 different experts. Among the 8 rows of one device no expert is named more than 4 times, and in every draw some device's rows name some expert exactly 4 times.
All inputs are finite; a program needn't handle non-finite values.
Results may differ from a plain program's by a relative error of at most 0.0057.
Values may be sent and summed in bfloat16 or wider, within the bound.
A program may use at most 64 MiB of HBM per device.

v0:
```python
import jax
import jax.numpy as jnp
from jax import lax
from jax.sharding import PartitionSpec as P

CAP = 4
META = 128


def pieces(w):
    hi = w.astype(jnp.bfloat16)
    rest = w - hi.astype(jnp.float32)
    mid = rest.astype(jnp.bfloat16)
    low = (rest - mid.astype(jnp.float32)).astype(jnp.bfloat16)
    return jnp.concatenate([hi, mid, low], axis=-1)


def per_device(tokens, route_weights, expert_ids, gate_weight, up_weight, down_weight):
    n_ep = lax.axis_size("ep")
    rows, width = tokens.shape
    named = expert_ids[:, :, None] == jnp.arange(n_ep, dtype=jnp.int32)[None, None, :]
    dense = jnp.sum(jnp.where(named, route_weights[:, :, None], 0.0), axis=1)
    eye = jnp.eye(rows, dtype=jnp.bfloat16)
    meta = jnp.concatenate([pieces(dense), eye], axis=1)
    meta = jnp.pad(meta, ((0, 0), (0, META - meta.shape[1])))
    sent = jnp.concatenate([tokens, meta], axis=1)
    got = lax.all_gather(sent, "ep", axis=0)
    me = lax.axis_index("ep")

    def weight_of(block):
        m = block[..., width:].astype(jnp.float32)
        part = [lax.dynamic_slice_in_dim(m, me + j * n_ep, 1, axis=-1) for j in range(3)]
        return (part[0] + part[1] + part[2])[..., 0]

    mask = weight_of(got) > 0
    slot = jnp.cumsum(mask.astype(jnp.int32), axis=1) - 1
    pick = mask[:, None, :] & (slot[:, None, :] == jnp.arange(CAP)[None, :, None])
    sel = jnp.einsum(
        "bst,btd->bsd", pick.astype(jnp.bfloat16), got, preferred_element_type=jnp.bfloat16
    )
    piece = lax.all_gather(sel, ("tp", "dp"), axis=0)
    x = piece[..., :width]
    gate = jnp.einsum("gbsd,df->gbsf", x, gate_weight[0], preferred_element_type=jnp.float32)
    up = jnp.einsum("gbsd,df->gbsf", x, up_weight[0], preferred_element_type=jnp.float32)
    hidden = (jax.nn.silu(gate) * up).astype(jnp.bfloat16)
    hidden = lax.all_gather(hidden, ("tp", "dp"), axis=3, tiled=True)
    out = jnp.einsum(
        "gbsf,fd->gbsd", hidden, down_weight[0], preferred_element_type=jnp.float32
    ).astype(jnp.bfloat16)
    code = piece[..., width + 3 * n_ep : width + 3 * n_ep + rows]
    w = weight_of(piece)
    w_tok = jnp.sum(code.astype(jnp.float32) * w[..., None], axis=2)
    back = jnp.einsum("gbst,gbsd->bgtd", code, out, preferred_element_type=jnp.float32)
    back = (back * jnp.swapaxes(w_tok, 0, 1)[..., None]).astype(jnp.bfloat16)
    flat = back.reshape(n_ep * back.shape[1] * rows, back.shape[3])
    summed = lax.psum_scatter(flat, "ep", scatter_dimension=0, tiled=True)
    summed = summed.reshape(back.shape[1], rows, back.shape[3])
    mine = lax.all_to_all(summed, ("tp", "dp"), split_axis=0, concat_axis=2, tiled=True)
    return mine[0]


def solution(mesh):
    tok = P(("groups", "ep", "tp", "dp"), None)
    wgt = P("ep", None, ("tp", "dp"))
    return jax.shard_map(
        per_device,
        mesh=mesh,
        in_specs=(tok, tok, tok, wgt, wgt, wgt),
        out_specs=tok,
        check_vma=False,
    )
```

profile of v0, /device:TPU:33, one launch (start us, length us, event | category | flops | bytes accessed | tf_op | source)
XLA Modules:
  0.0 466.4 jit_solution(3061447939570187865)
XLA Ops:
  6.5 0.0 copy-start
  6.6 0.0 all-gather.8.cloned.1.call-start
  6.6 0.9 select_reduce_fusion
  7.5 0.1 fusion.33
  7.6 1.5 pad_maximum_fusion
  9.1 0.1 all-gather.8.cloned.1.call-update
  9.1 0.1 all-gather.10.cloned.1.call-start
  9.2 142.7 %all-gather.8.cloned.1.call-done = bf16[256,5248]{1,0:T(8,128)(2,1)} async-done(((bf16[8,5248]{1,0:T(8,128)(2,1)}), bf16[256,5248]{1,0:T(8,128)(2,1)}) %all-gather.8.cloned.1.call-update) | async-done | bytes 2686992 | tf_op jit(solution)/shard_map/all_gather | solution.py:27
  151.9 0.8 slice.16
  152.8 0.2 copy.60
  153.1 0.1 copy.49
  153.2 0.1 copy.50
  153.2 3.7 fusion.20
  156.9 0.1 all-gather.10.cloned.1.call-update
  157.0 0.0 copy-start.2
  157.0 0.1 all-gather.6.cloned.1.call-start
  157.1 88.1 %all-gather.10.cloned.1.call-done = bf16[256,4,5248]{2,1,0:T(4,128)(2,1)} async-done(((bf16[32,4,5248]{2,1,0:T(4,128)(2,1)}), bf16[256,4,5248]{2,1,0:T(4,128)(2,1)}) %all-gather.10.cloned.1.call-update) | async-done | bytes 10747920 | tf_op jit(solution)/shard_map/all_gather | solution.py:41
  245.2 7.1 %copy.51 = bf16[256,4,5248]{2,0,1:T(8,128)(2,1)S(1)} copy(bf16[256,4,5248]{2,1,0:T(4,128)(2,1)} %all-gather.10.cloned.1.call-done) | data formatting | bytes 21495808 | tf_op jit(solution)/shard_map/all_gather | solution.py:41
  252.4 0.0 copy-start.1
  252.4 0.0 copy-done.2
  252.4 0.0 copy-start.3
  252.4 2.9 fusion.2
  255.3 1.2 copy-done.1
  256.4 0.0 copy-done.3
  256.5 3.7 fusion.13
  260.2 0.1 all-gather.6.cloned.1.call-update
  260.2 0.1 reduce-scatter.2.cloned.1.call-start
  260.3 1.1 slice.17
  261.4 1.0 slice_convert_fusion
  262.4 0.5 dynamic-slice_add_fusion
  262.9 1.6 copy.59
  264.5 0.5 multiply_reduce_fusion
  265.0 39.3 %all-gather.6.cloned.1.call-done = bf16[8,32,4,1024]{3,1,2,0:T(8,128)(2,1)} async-done(((bf16[8,32,4,128]{3,1,2,0:T(8,128)(2,1)}), bf16[8,32,4,1024]{3,1,2,0:T(8,128)(2,1)}) %all-gather.6.cloned.1.call-update) | async-done | bytes 2097168 | tf_op jit(solution)/shard_map/all_gather | solution.py:46
  304.4 0.0 copy-done
  304.4 3.4 convolution_convert_fusion
  307.8 3.0 multiply_convert_fusion
  310.7 0.1 reduce-scatter.2.cloned.1.call-update
  310.8 117.5 %reduce-scatter.2.cloned.1.call-done = bf16[64,640]{1,0:T(8,128)(2,1)} async-done(((bf16[2048,640]{1,0:T(8,128)(2,1)}), bf16[64,640]{1,0:T(8,128)(2,1)}) %reduce-scatter.2.cloned.1.call-update) | async-done | bytes 81936 | tf_op jit(solution)/shard_map/reduce_scatter | solution.py:56
  428.3 30.9 %all_to_all.15 = bf16[8,8,640]{2,1,0:T(8,128)(2,1)S(1)} all-to-all(bf16[8,8,640]{2,1,0:T(8,128)(2,1)} %bitcast.51), channel_id=1, replica_groups=mesh['groups'=2,'ep'=32,'tp'=4,'dp'=2] {'tp','dp'}, dimensions={0} | all-to-all | bytes 163840 | tf_op jit(solution)/shard_map/all_to_all | solution.py:58
  459.2 0.6 copy.77
  (6 shorter events, 0.1 us)
Async XLA Ops:
  6.5 297.8 %copy-start = (bf16[1,1024,640]{2,1,0:T(8,128)(2,1)S(1)}, bf16[1,1024,640]{2,1,0:T(8,128)(2,1)}, u32[]{:S(2)}) copy-start(bf16[1,1024,640]{2,1,0:T(8,128)(2,1)} %param.11) | copy-start | bytes 3932164
  6.6 145.4 %all-gather.8.cloned.1.call-start = ((), (), s32[]{:S(2)}) async-start(), calls=%async_computation.4 | async-start | bytes 2770944 | tf_op jit(solution)/shard_map/all_gather | solution.py:27
  9.1 236.1 %all-gather.10.cloned.1.call-start = ((), (), s32[]{:S(2)}) async-start(), calls=%async_computation.5 | async-start | bytes 12091392 | tf_op jit(solution)/shard_map/all_gather | solution.py:41
  157.0 95.4 %copy-start.2 = (bf16[1,5120,128]{2,1,0:T(8,128)(2,1)S(1)}, bf16[1,5120,128]{2,1,0:T(8,128)(2,1)}, u32[]{:S(2)}) copy-start(bf16[1,5120,128]{2,1,0:T(8,128)(2,1)} %param.9) | copy-start | bytes 3932164
  157.0 147.4 %all-gather.6.cloned.1.call-start = ((), (), s32[]{:S(2)}) async-start(), calls=%async_computation.2 | async-start | bytes 2359296 | tf_op jit(solution)/shard_map/all_gather | solution.py:46
  252.4 4.1 copy-start.1
  252.4 4.1 copy-start.3
  260.2 168.0 %reduce-scatter.2.cloned.1.call-start = ((), (), s32[]{:S(2)}) async-start(), calls=%async_computation.3 | async-start | bytes 2703360 | tf_op jit(solution)/shard_map/reduce_scatter | solution.py:56
Sparse Core Ops, SparseCore 0:
  9.4 142.4 all-gather.7
  157.1 88.0 all-gather.9
  260.4 43.9 all-gather.5
  310.9 117.3 reduce-scatter.1
where the time goes:
time: 467 us; the launch traced here: 466 us
  waiting for transfers between devices  388 us (83%)
  blocking collectives  30.9 us (7%)
  matrix products  16.6 us (4%)
  between operations  13.3 us (3%)
  local copies, waits for them, and re-layouts  12.9 us (3%)
    all_gather x1, waiting for transfers between devices, per_device(): got = lax.all_gather(sent, 'ep', axis=0)  143 us
    reduce_scatter x1, waiting for transfers between devices, per_device(): summed = lax.psum_scatter(flat, 'ep', scatter_dimension=0, tiled=True)  117 us
    all_gather x1, waiting for transfers between devices, per_device(): piece = lax.all_gather(sel, ('tp', 'dp'), axis=0)  88.1 us
    all_gather x1, waiting for transfers between devices, per_device(): hidden = lax.all_gather(hidden, ('tp', 'dp'), axis=3, tiled=True)  39.3 us
    all_to_all x1, blocking collectives, per_device(): lax.all_to_all(summed, ('tp', 'dp'), split_axis=0, concat_axis=2, tiled=T...  30.9 us
  transfers between devices with their start and end apart: 4, of which 4 were waited for; matrix products, arithmetic and copies ran while one was open for 1% of the time, Pallas kernels for 0%

commit v1 on v0

--- a/solution.py
+++ b/solution.py
@@ -43,7 +43,10 @@
     gate = jnp.einsum("gbsd,df->gbsf", x, gate_weight[0], preferred_element_type=jnp.float32)
     up = jnp.einsum("gbsd,df->gbsf", x, up_weight[0], preferred_element_type=jnp.float32)
     hidden = (jax.nn.silu(gate) * up).astype(jnp.bfloat16)
-    hidden = lax.all_gather(hidden, ("tp", "dp"), axis=3, tiled=True)
+    size = lax.axis_size(("tp", "dp"))
+    shards = jnp.stack([hidden for _ in range(size)])
+    shards = lax.all_to_all(shards, ("tp", "dp"), split_axis=0, concat_axis=0)
+    hidden = jnp.concatenate(shards, axis=3)
     out = jnp.einsum(
         "gbsf,fd->gbsd", hidden, down_weight[0], preferred_element_type=jnp.float32
     ).astype(jnp.bfloat16)

time: 467 us -> 452 us (0.968)
  waiting for transfers between devices: 388 us -> 366 us
    all_gather x1 -> x0, waiting for transfers between devices: 39.3 us -> none  [per_device(): hidden = lax.all_gather(hidden, ('tp', 'dp'), axis=3, tiled=True)]
    all_to_all x0 -> x1, waiting for transfers between devices: none -> 17.4 us  [per_device(): shards = lax.all_to_all(shards, ('tp', 'dp'), split_axis=0, concat_axis=0)]
  transfers between devices with their start and end apart: 4 -> 4, of which waited for: 4 -> 4; matrix products, arithmetic and copies ran while one was open for 1% -> 2% of each run, Pallas kernels for 0% -> 0%
where the time goes in v1:
time: 452 us
  waiting for transfers between devices  366 us (81%)
  blocking collectives  30.6 us (7%)
  local copies, waits for them, and re-layouts  16.5 us (4%)
  matrix products  14.4 us (3%)
  between operations  13.3 us (3%)
  other arithmetic  6.99 us (2%)
    all_gather x1, waiting for transfers between devices, per_device(): got = lax.all_gather(sent, 'ep', axis=0)  143 us
    reduce_scatter x1, waiting for transfers between devices, per_device(): summed = lax.psum_scatter(flat, 'ep', scatter_dimension=0, tiled=True)  117 us
    all_gather x1, waiting for transfers between devices, per_device(): piece = lax.all_gather(sel, ('tp', 'dp'), axis=0)  88.2 us
    all_to_all x1, blocking collectives, per_device(): lax.all_to_all(summed, ('tp', 'dp'), split_axis=0, concat_axis=2, tiled=T...  30.6 us
    all_to_all x1, waiting for transfers between devices, per_device(): shards = lax.all_to_all(shards, ('tp', 'dp'), split_axis=0, concat_axis=0)  17.4 us
  transfers between devices with their start and end apart: 4, of which 4 were waited for; matrix products, arithmetic and copies ran while one was open for 2% of the time, Pallas kernels for 0%

profile of v1, /device:TPU:33, one launch (start us, length us, event | category | flops | bytes accessed | tf_op | source)
XLA Modules:
  0.0 451.6 jit_solution(490138838270041111)
XLA Ops:
  6.5 0.0 copy-start
  6.6 0.0 all-gather.5.cloned.1.call-start
  6.6 0.9 select_reduce_fusion
  7.5 0.1 fusion.39
  7.6 1.5 pad_maximum_fusion
  9.1 0.1 all-gather.5.cloned.1.call-update
  9.1 0.1 all-gather.7.cloned.1.call-start
  9.2 142.7 %all-gather.5.cloned.1.call-done = bf16[256,5248]{1,0:T(8,128)(2,1)} async-done(((bf16[8,5248]{1,0:T(8,128)(2,1)}), bf16[256,5248]{1,0:T(8,128)(2,1)}) %all-gather.5.cloned.1.call-update) | async-done | bytes 2686992 | tf_op jit(solution)/shard_map/all_gather | solution.py:27
  151.9 0.8 slice.16
  152.8 0.2 copy.66
  153.1 0.1 copy.54
  153.2 0.1 copy.55
  153.2 3.7 fusion.26
  156.9 0.1 all-gather.7.cloned.1.call-update
  157.0 0.0 copy-start.4
  157.0 88.2 %all-gather.7.cloned.1.call-done = bf16[256,4,5248]{2,1,0:T(4,128)(2,1)} async-done(((bf16[32,4,5248]{2,1,0:T(4,128)(2,1)}), bf16[256,4,5248]{2,1,0:T(4,128)(2,1)}) %all-gather.7.cloned.1.call-update) | async-done | bytes 10747920 | tf_op jit(solution)/shard_map/all_gather | solution.py:41
  245.2 7.1 %copy.56 = bf16[256,4,5248]{2,0,1:T(8,128)(2,1)S(1)} copy(bf16[256,4,5248]{2,1,0:T(4,128)(2,1)} %all-gather.7.cloned.1.call-done) | data formatting | bytes 21495808 | tf_op jit(solution)/shard_map/all_gather | solution.py:41
  252.4 0.0 copy-start.1
  252.4 0.0 copy-done.4
  252.4 0.0 copy-start.5
  252.4 2.9 fusion.2
  255.3 1.2 copy-done.1
  256.5 0.0 copy-done.5
  256.5 3.1 fusion.19
  259.5 1.8 stack.2
  261.4 3.8 all-to-all-start
  265.2 0.0 reduce-scatter.2.cloned.1.call-start
  265.2 1.8 slice.17
  267.0 1.0 slice_convert_fusion
  268.0 1.3 dynamic-slice_add_fusion
  269.2 2.6 copy.65
  271.9 2.1 multiply_reduce_fusion
  274.0 0.0 copy-start.3
  274.0 17.4 %all-to-all-done = bf16[8,8,32,4,128]{4,2,3,1,0:T(8,128)(2,1)S(1)} async-done(((bf16[8,8,32,4,128]{4,2,3,1,0:T(8,128)(2,1)}), bf16[8,8,32,4,128]{4,2,3,1,0:T(8,128)(2,1)S(1)}, u32[]{:S(2)}, u32[]{:S(2)}) %all-to-all-start) | async-done | bytes 2097184 | tf_op jit(solution)/shard_map/all_to_all | solution.py:48
  291.4 0.0 copy-done
  291.4 0.0 copy-start.2
  291.5 1.8 fusion.7
  293.2 0.0 copy-done.3
  293.3 0.0 copy-done.2
  293.3 3.0 multiply_convert_fusion
  296.2 0.1 reduce-scatter.2.cloned.1.call-update
  296.3 117.5 %reduce-scatter.2.cloned.1.call-done = bf16[64,640]{1,0:T(8,128)(2,1)} async-done(((bf16[2048,640]{1,0:T(8,128)(2,1)}), bf16[64,640]{1,0:T(8,128)(2,1)}) %reduce-scatter.2.cloned.1.call-update) | async-done | bytes 81936 | tf_op jit(solution)/shard_map/reduce_scatter | solution.py:59
  413.8 30.6 %all_to_all.20 = bf16[8,8,640]{2,1,0:T(8,128)(2,1)S(1)} all-to-all(bf16[8,8,640]{2,1,0:T(8,128)(2,1)} %bitcast.60), channel_id=1, replica_groups=mesh['groups'=2,'ep'=32,'tp'=4,'dp'=2] {'tp','dp'}, dimensions={0} | all-to-all | bytes 163840 | tf_op jit(solution)/shard_map/all_to_all | solution.py:61
  444.4 0.6 copy.90
  (6 shorter events, 0.1 us)
Async XLA Ops:
  6.5 284.9 %copy-start = (bf16[1,1024,640]{2,1,0:T(8,128)(2,1)S(1)}, bf16[1,1024,640]{2,1,0:T(8,128)(2,1)}, u32[]{:S(2)}) copy-start(bf16[1,1024,640]{2,1,0:T(8,128)(2,1)} %param.11) | copy-start | bytes 3932164
  6.6 145.4 %all-gather.5.cloned.1.call-start = ((), (), s32[]{:S(2)}) async-start(), calls=%async_computation.4 | async-start | bytes 2770944 | tf_op jit(solution)/shard_map/all_gather | solution.py:27
  9.1 236.1 %all-gather.7.cloned.1.call-start = ((), (), s32[]{:S(2)}) async-start(), calls=%async_computation.5 | async-start | bytes 12091392 | tf_op jit(solution)/shard_map/all_gather | solution.py:41
  157.0 95.4 %copy-start.4 = (bf16[1,5120,128]{2,1,0:T(8,128)(2,1)S(1)}, bf16[1,5120,128]{2,1,0:T(8,128)(2,1)}, u32[]{:S(2)}) copy-start(bf16[1,5120,128]{2,1,0:T(8,128)(2,1)} %param.9) | copy-start | bytes 3932164
  252.4 4.1 copy-start.1
  252.4 4.1 copy-start.5
  261.4 30.1 %all-to-all-start = ((bf16[8,8,32,4,128]{4,2,3,1,0:T(8,128)(2,1)}), bf16[8,8,32,4,128]{4,2,3,1,0:T(8,128)(2,1)S(1)}, u32[]{:S(2)}, u32[]{:S(2)}) async-start(bf16[8,8,32,4,128]{4,2,3,1,0:T(8,128)(2,1)} %stack.2), calls=%async_computation | async-start | bytes 4194304 | tf_op jit(solution)/shard_map/all_to_all | solution.py:48
  265.2 148.6 %reduce-scatter.2.cloned.1.call-start = ((), (), s32[]{:S(2)}) async-start(), calls=%async_computation.3 | async-start | bytes 2703360 | tf_op jit(solution)/shard_map/reduce_scatter | solution.py:59
  274.0 19.3 %copy-start.3 = (f32[8,32,8]{2,0,1:T(8,128)S(1)}, f32[8,32,8]{2,0,1:T(8,128)}, u32[]{:S(2)}) copy-start(f32[8,32,8]{2,0,1:T(8,128)} %multiply_reduce_fusion) | copy-start | bytes 24580
  291.4 1.8 copy-start.2
Sparse Core Ops, SparseCore 0:
  9.4 142.4 all-gather.4
  157.1 88.0 all-gather.6
  296.4 117.3 reduce-scatter.1
